TPU v7x, 32 devices: a whole 2x2x4 slice. The times are simulated.
32 devices in a mesh: dp: 16 (over z, y, x), expert: 2 (over core).
Axes of the slice: x: 2, y: 2, z: 4, core: 2. Of those that a mesh axis runs over, the one named last changes fastest.
Arguments:
- master: float32 [2, 7168, 2048], P('expert', 'dp'), may hold values from -6 to 6
- first_moment: float32 [2, 7168, 2048], P('expert', 'dp'), may hold values from -0.06 to 0.06
- second_moment: float32 [2, 7168, 2048], P('expert', 'dp'), may hold values from 1e-05 to 0.001
- rotation: int32 [4, 16, 1], replicated, may hold values from 0 to 15; in each aligned block of 16 rows (0 to 15, 16 to 31, ..., all dimensions but the last counted through in order) at most 3 rows name the same one
- assignment: int32 [64], replicated, may hold values from 0 to 63, each once
Outputs:
- saved_master: float32 [2, 64, 3, 1792, 128], P('expert', 'dp')
- saved_update: float32 [2, 64, 3, 1792, 128], P('expert', 'dp')
- checksums: float32 [2, 2, 64], replicated
Inputs may be any that keep to these rules, and one draw needn't show every extreme that they name: rotation[r, j, 0] is the dp index that writes span j of round r; within one round no index is named more than 3 times, and in some round one index is named exactly 3 times. `assignment`: a permutation of the spans' checksum slots.
All inputs are finite; a program needn't handle non-finite values.
Results may differ from a plain program's by a relative error of at most 0.00002.
Values sent between devices are 32-bit elements; how exact they have to be, the bound alone decides.
A program may use at most 128 MiB of HBM per device.

v0:
```python
import math

import jax
import jax.numpy as jnp
from jax import lax
from jax.sharding import PartitionSpec as P

LANE = 128
MOST = 3
STEP = 20


BETA_ONE = 0.9
BETA_TWO = 0.95
EPSILON = 1e-08


def scaled_moment(first_part, second_part):
    corr_one = 1.0 - BETA_ONE**STEP
    corr_two = 1.0 - BETA_TWO**STEP
    return first_part / corr_one / (jnp.sqrt(second_part / corr_two) + EPSILON)


def slot_table(rotation, dp_count, most_slots):
    owners = rotation[:, :, 0]
    span_ids = jnp.arange(dp_count, dtype=jnp.int32)
    same_writer = owners[:, :, None] == owners[:, None, :]
    before = span_ids[None, :] < span_ids[:, None]
    slot_rank = jnp.sum((same_writer & before[None]).astype(jnp.int32), axis=2)
    writers = jnp.arange(dp_count, dtype=jnp.int32)
    slot_ids = jnp.arange(most_slots, dtype=jnp.int32)
    matches = (owners[:, None, None, :] == writers[None, None, :, None]) & (
        slot_rank[:, None, None, :] == slot_ids[None, :, None, None]
    )
    matches = matches.astype(jnp.int32)
    found_any = jnp.sum(matches, axis=3)
    picked = jnp.sum(matches * span_ids, axis=3)
    return picked + (1 - found_any) * dp_count


def position_weights(line_ids, per_row, lane_count):
    row_ids = line_ids // per_row
    col_ids = line_ids % per_row * lane_count
    lane_ids = jnp.arange(lane_count, dtype=jnp.int32)
    pattern = (row_ids[..., None] * 5 + (col_ids[..., None] + lane_ids) * 3) % 11
    return 1.0 + pattern.astype(jnp.float32) / 10.0


def deliver_slots(send_parts):
    return (
        lax.all_to_all(send_parts[0], "dp", split_axis=1, concat_axis=1, tiled=True),
        lax.all_to_all(send_parts[1], "dp", split_axis=1, concat_axis=1, tiled=True),
    )


def shards(master, first_moment, second_moment, rotation, assignment):
    dp_count = lax.axis_size("dp")
    group_count = lax.axis_size("expert")
    position = lax.axis_index("dp")
    group_id = lax.axis_index("expert")
    round_count = rotation.shape[0]
    rows_here = master.shape[1]
    lane_count = LANE
    per_row = master.shape[2] // lane_count
    lines_device = rows_here * per_row
    piece_len = lines_device // (round_count * dp_count)
    inv_count = 1.0 / math.sqrt(dp_count * piece_len * lane_count)
    table = slot_table(rotation, dp_count, MOST)

    def line_pieces(field_in):
        return field_in.reshape(round_count, dp_count, piece_len, lane_count)

    def padded_pieces(line_view):
        return jnp.concatenate(
            [line_view, jnp.zeros((round_count, 1, piece_len, lane_count), line_view.dtype)], axis=1
        )

    update = scaled_moment(first_moment, second_moment)
    master_lines = line_pieces(master)
    update_lines = line_pieces(update)
    local_lines = position * lines_device + jnp.arange(lines_device, dtype=jnp.int32).reshape(
        round_count, dp_count, piece_len
    )
    weights = position_weights(local_lines, per_row, lane_count)
    master_sums = (
        jnp.sum(master_lines * weights, axis=(2, 3)).reshape(round_count * dp_count) * inv_count
    )
    update_sums = (
        jnp.sum(update_lines * weights, axis=(2, 3)).reshape(round_count * dp_count) * inv_count
    )
    sources = (padded_pieces(master_lines), padded_pieces(update_lines))
    results = []
    for round_idx in range(round_count):
        send_parts = tuple((source[round_idx][table[round_idx]] for source in sources))
        results.append(deliver_slots(send_parts))
    saved_master = jnp.stack([outcome[0] for outcome in results])
    saved_update = jnp.stack([outcome[1] for outcome in results])
    span_count = assignment.shape[0]
    slot_ids = jnp.arange(span_count, dtype=jnp.int32)
    permuting = (assignment[:, None] == slot_ids[None, :]).astype(jnp.float32)
    both_sums = jnp.stack([master_sums, update_sums])
    placed_sums = jnp.sum(both_sums[:, :, None] * permuting[None], axis=1)
    in_slot = (jnp.arange(group_count, dtype=jnp.int32) == group_id).astype(jnp.float32)
    contribution = in_slot[:, None, None] * placed_sums[None]
    checksums = lax.psum(contribution, ("dp", "expert"))
    shape_out = (1, round_count, MOST, dp_count * piece_len, lane_count)
    return (saved_master.reshape(shape_out), saved_update.reshape(shape_out), checksums)


def solution(mesh):
    placed = (P("expert", "dp", None), P("expert", "dp", None), P("expert", "dp", None), P(), P())
    return jax.shard_map(
        shards,
        mesh=mesh,
        in_specs=placed,
        out_specs=(P("expert", "dp", None, None, None), P("expert", "dp", None, None, None), P()),
        check_vma=False,
    )
```

profile of v0, /device:TPU:0, one launch (start us, length us, event | category | flops | bytes accessed | tf_op | source)
XLA Modules:
  0.0 604.0 jit_solution(13981330019251807137)
XLA Ops:
  3.0 4.7 reshape.309
  13.2 3.6 copy.40
  16.8 8.4 %all-to-all-start = ((f32[3,16,112,128]{3,2,0,1:T(8,128)}), f32[3,16,112,128]{3,2,0,1:T(8,128)}, u32[]{:S(2)}, u32[]{:S(2)}) async-start(f32[3,16,112,128]{3,2,0,1:T(8,128)} %copy.40), calls=%async_computation | async-start | bytes 5505024 | tf_op jit(solution)/shard_map/all_to_all | solution.py:51
  25.2 6.4 %add_divide_fusion = f32[1,448,2048]{2,1,0:T(8,128)} fusion(f32[1,448,2048]{2,1,0:T(8,128)} %param.7, f32[1,448,2048]{2,1,0:T(8,128)} %param.6), kind=kLoop, calls=%fused_computation.19 | loop fusion | flops 3670016 | bytes 11010048 | tf_op jit(solution)/shard_map/div | solution.py:21
  31.6 4.7 reshape.310
  36.3 3.7 fusion.10
  46.9 32.4 %all-to-all-done = f32[3,16,112,128]{3,2,0,1:T(8,128)} async-done(((f32[3,16,112,128]{3,2,0,1:T(8,128)}), f32[3,16,112,128]{3,2,0,1:T(8,128)}, u32[]{:S(2)}, u32[]{:S(2)}) %all-to-all-start) | async-done | bytes 2752544 | tf_op jit(solution)/shard_map/all_to_all | solution.py:51
  79.4 13.2 %all-to-all-start.4 = ((f32[3,16,112,128]{3,2,0,1:T(8,128)}), f32[3,16,112,128]{3,2,0,1:T(8,128)}, u32[]{:S(2)}, u32[]{:S(2)}) async-start(f32[3,16,112,128]{3,2,0,1:T(8,128)} %copy.48), calls=%async_computation.4 | async-start | bytes 5505024 | tf_op jit(solution)/shard_map/all_to_all | solution.py:52
  96.1 3.6 copy.42
  99.7 46.7 %all-to-all-done.4 = f32[3,16,112,128]{3,2,0,1:T(8,128)} async-done(((f32[3,16,112,128]{3,2,0,1:T(8,128)}), f32[3,16,112,128]{3,2,0,1:T(8,128)}, u32[]{:S(2)}, u32[]{:S(2)}) %all-to-all-start.4) | async-done | bytes 2752544 | tf_op jit(solution)/shard_map/all_to_all | solution.py:52
  146.4 12.6 %all-to-all-start.1 = ((f32[3,16,112,128]{3,2,0,1:T(8,128)}), f32[3,16,112,128]{3,2,0,1:T(8,128)}, u32[]{:S(2)}, u32[]{:S(2)}) async-start(f32[3,16,112,128]{3,2,0,1:T(8,128)} %copy.42), calls=%async_computation.1 | async-start | bytes 5505024 | tf_op jit(solution)/shard_map/all_to_all | solution.py:51
  165.9 46.9 %all-to-all-done.1 = f32[3,16,112,128]{3,2,0,1:T(8,128)} async-done(((f32[3,16,112,128]{3,2,0,1:T(8,128)}), f32[3,16,112,128]{3,2,0,1:T(8,128)}, u32[]{:S(2)}, u32[]{:S(2)}) %all-to-all-start.1) | async-done | bytes 2752544 | tf_op jit(solution)/shard_map/all_to_all | solution.py:51
  212.9 12.5 %all-to-all-start.5 = ((f32[3,16,112,128]{3,2,0,1:T(8,128)}), f32[3,16,112,128]{3,2,0,1:T(8,128)}, u32[]{:S(2)}, u32[]{:S(2)}) async-start(f32[3,16,112,128]{3,2,0,1:T(8,128)} %copy.50), calls=%async_computation.5 | async-start | bytes 5505024 | tf_op jit(solution)/shard_map/all_to_all | solution.py:52
  227.8 3.5 copy.44
  231.3 48.0 %all-to-all-done.5 = f32[3,16,112,128]{3,2,0,1:T(8,128)} async-done(((f32[3,16,112,128]{3,2,0,1:T(8,128)}), f32[3,16,112,128]{3,2,0,1:T(8,128)}, u32[]{:S(2)}, u32[]{:S(2)}) %all-to-all-start.5) | async-done | bytes 2752544 | tf_op jit(solution)/shard_map/all_to_all | solution.py:52
  279.2 12.5 %all-to-all-start.2 = ((f32[3,16,112,128]{3,2,0,1:T(8,128)}), f32[3,16,112,128]{3,2,0,1:T(8,128)}, u32[]{:S(2)}, u32[]{:S(2)}) async-start(f32[3,16,112,128]{3,2,0,1:T(8,128)} %copy.44), calls=%async_computation.2 | async-start | bytes 5505024 | tf_op jit(solution)/shard_map/all_to_all | solution.py:51
  294.0 3.5 copy.52
  297.5 48.0 %all-to-all-done.2 = f32[3,16,112,128]{3,2,0,1:T(8,128)} async-done(((f32[3,16,112,128]{3,2,0,1:T(8,128)}), f32[3,16,112,128]{3,2,0,1:T(8,128)}, u32[]{:S(2)}, u32[]{:S(2)}) %all-to-all-start.2) | async-done | bytes 2752544 | tf_op jit(solution)/shard_map/all_to_all | solution.py:51
  345.5 12.5 %all-to-all-start.6 = ((f32[3,16,112,128]{3,2,0,1:T(8,128)}), f32[3,16,112,128]{3,2,0,1:T(8,128)}, u32[]{:S(2)}, u32[]{:S(2)}) async-start(f32[3,16,112,128]{3,2,0,1:T(8,128)} %copy.52), calls=%async_computation.6 | async-start | bytes 5505024 | tf_op jit(solution)/shard_map/all_to_all | solution.py:52
  360.3 3.5 copy.46
  363.9 47.9 %all-to-all-done.6 = f32[3,16,112,128]{3,2,0,1:T(8,128)} async-done(((f32[3,16,112,128]{3,2,0,1:T(8,128)}), f32[3,16,112,128]{3,2,0,1:T(8,128)}, u32[]{:S(2)}, u32[]{:S(2)}) %all-to-all-start.6) | async-done | bytes 2752544 | tf_op jit(solution)/shard_map/all_to_all | solution.py:52
  411.8 12.5 %all-to-all-start.3 = ((f32[3,16,112,128]{3,2,0,1:T(8,128)}), f32[3,16,112,128]{3,2,0,1:T(8,128)}, u32[]{:S(2)}, u32[]{:S(2)}) async-start(f32[3,16,112,128]{3,2,0,1:T(8,128)} %copy.46), calls=%async_computation.3 | async-start | bytes 5505024 | tf_op jit(solution)/shard_map/all_to_all | solution.py:51
  426.5 3.5 copy.54
  430.1 48.0 %all-to-all-done.3 = f32[3,16,112,128]{3,2,0,1:T(8,128)} async-done(((f32[3,16,112,128]{3,2,0,1:T(8,128)}), f32[3,16,112,128]{3,2,0,1:T(8,128)}, u32[]{:S(2)}, u32[]{:S(2)}) %all-to-all-start.3) | async-done | bytes 2752544 | tf_op jit(solution)/shard_map/all_to_all | solution.py:51
  478.1 12.4 %all-to-all-start.7 = ((f32[3,16,112,128]{3,2,0,1:T(8,128)}), f32[3,16,112,128]{3,2,0,1:T(8,128)S(1)}, u32[]{:S(2)}, u32[]{:S(2)}) async-start(f32[3,16,112,128]{3,2,0,1:T(8,128)} %copy.54), calls=%async_computation.7 | async-start | bytes 5505024 | tf_op jit(solution)/shard_map/all_to_all | solution.py:52
  490.6 13.4 %multiply_reduce_fusion.1 = (f32[4,16]{1,0:T(4,128)S(1)}, f32[4,16]{1,0:T(4,128)S(1)}) fusion(f32[4,16,112,128]{3,2,1,0:T(8,128)} %reshape.309, s32[4,16,112]{2,1,0:T(8,128)S(1)} %get-tuple-element.24, s32[4,16,112]{2,1,0:T(8,128)S(1)} %get-tuple-element.23, f32[4,16,112,128]{3,2,1,0:T(8,128)} %reshape.310), kind=kLoop, calls=%fused_computation.15 | loop fusion | flops 14679936 | bytes 7397888 | tf_op jit(solution)/shard_map/reduce_sum | solution.py:86
  504.5 68.0 %psum.7 = f32[2,2,64]{2,1,0:T(2,128)} all-reduce(f32[2,2,64]{2,1,0:T(2,128)S(1)} %broadcast_multiply_fusion), channel_id=1, replica_groups=mesh['dp'=16,'expert'=2] {'dp','expert'}, use_global_device_ids=true, to_apply=%region_6.7 | all-reduce | flops 256 | bytes 2048 | tf_op jit(solution)/shard_map/psum | solution.py:105
  574.5 3.6 copy.49
  580.0 3.6 copy.51
  585.6 3.6 copy.53
  591.2 4.5 pad_maximum_fusion
  598.3 5.7 pad_maximum_fusion.1
  (52 shorter events, 45.5 us)
Async XLA Ops:
  16.8 62.6 %all-to-all-start = ((f32[3,16,112,128]{3,2,0,1:T(8,128)}), f32[3,16,112,128]{3,2,0,1:T(8,128)}, u32[]{:S(2)}, u32[]{:S(2)}) async-start(f32[3,16,112,128]{3,2,0,1:T(8,128)} %copy.40), calls=%async_computation | async-start | bytes 5505024 | tf_op jit(solution)/shard_map/all_to_all | solution.py:51
  79.4 67.1 %all-to-all-start.4 = ((f32[3,16,112,128]{3,2,0,1:T(8,128)}), f32[3,16,112,128]{3,2,0,1:T(8,128)}, u32[]{:S(2)}, u32[]{:S(2)}) async-start(f32[3,16,112,128]{3,2,0,1:T(8,128)} %copy.48), calls=%async_computation.4 | async-start | bytes 5505024 | tf_op jit(solution)/shard_map/all_to_all | solution.py:52
  146.4 66.4 %all-to-all-start.1 = ((f32[3,16,112,128]{3,2,0,1:T(8,128)}), f32[3,16,112,128]{3,2,0,1:T(8,128)}, u32[]{:S(2)}, u32[]{:S(2)}) async-start(f32[3,16,112,128]{3,2,0,1:T(8,128)} %copy.42), calls=%async_computation.1 | async-start | bytes 5505024 | tf_op jit(solution)/shard_map/all_to_all | solution.py:51
  212.9 66.4 %all-to-all-start.5 = ((f32[3,16,112,128]{3,2,0,1:T(8,128)}), f32[3,16,112,128]{3,2,0,1:T(8,128)}, u32[]{:S(2)}, u32[]{:S(2)}) async-start(f32[3,16,112,128]{3,2,0,1:T(8,128)} %copy.50), calls=%async_computation.5 | async-start | bytes 5505024 | tf_op jit(solution)/shard_map/all_to_all | solution.py:52
  231.2 60.5 %copy-start = (f32[17,112,128]{2,1,0:T(8,128)S(1)}, f32[17,112,128]{2,1,0:T(8,128)}, u32[]{:S(2)}) copy-start(f32[17,112,128]{2,1,0:T(8,128)} %get-tuple-element.9) | copy-start | bytes 2924548
  279.2 66.3 %all-to-all-start.2 = ((f32[3,16,112,128]{3,2,0,1:T(8,128)}), f32[3,16,112,128]{3,2,0,1:T(8,128)}, u32[]{:S(2)}, u32[]{:S(2)}) async-start(f32[3,16,112,128]{3,2,0,1:T(8,128)} %copy.44), calls=%async_computation.2 | async-start | bytes 5505024 | tf_op jit(solution)/shard_map/all_to_all | solution.py:51
  345.5 66.3 %all-to-all-start.6 = ((f32[3,16,112,128]{3,2,0,1:T(8,128)}), f32[3,16,112,128]{3,2,0,1:T(8,128)}, u32[]{:S(2)}, u32[]{:S(2)}) async-start(f32[3,16,112,128]{3,2,0,1:T(8,128)} %copy.52), calls=%async_computation.6 | async-start | bytes 5505024 | tf_op jit(solution)/shard_map/all_to_all | solution.py:52
  411.8 66.3 %all-to-all-start.3 = ((f32[3,16,112,128]{3,2,0,1:T(8,128)}), f32[3,16,112,128]{3,2,0,1:T(8,128)}, u32[]{:S(2)}, u32[]{:S(2)}) async-start(f32[3,16,112,128]{3,2,0,1:T(8,128)} %copy.46), calls=%async_computation.3 | async-start | bytes 5505024 | tf_op jit(solution)/shard_map/all_to_all | solution.py:51
  478.1 117.7 %all-to-all-start.7 = ((f32[3,16,112,128]{3,2,0,1:T(8,128)}), f32[3,16,112,128]{3,2,0,1:T(8,128)S(1)}, u32[]{:S(2)}, u32[]{:S(2)}) async-start(f32[3,16,112,128]{3,2,0,1:T(8,128)} %copy.54), calls=%async_computation.7 | async-start | bytes 5505024 | tf_op jit(solution)/shard_map/all_to_all | solution.py:52
  490.5 13.7 %copy-start.3 = (s32[64]{0:T(128)S(1)}, s32[64]{0:T(128)}, u32[]{:S(2)}) copy-start(s32[64]{0:T(128)} %param.9) | copy-start | bytes 772
  595.7 1.8 copy-start.1
  595.7 2.6 copy-start.2
where the time goes:
time: 606 us; the launch traced here: 604 us
  waiting for transfers between devices  318 us (52%)
  starting transfers between devices  96.6 us (16%)
  local copies, waits for them, and re-layouts  88 us (15%)
  blocking collectives  68 us (11%)
  other arithmetic  32.6 us (5%)
    all_to_all x4, waiting for transfers between devices, deliver_slots(): lax.all_to_all(send_parts[0], 'dp', split_axis=1, concat_axis=1, tiled=True)  175 us
    all_to_all x4, waiting for transfers between devices, deliver_slots(): lax.all_to_all(send_parts[1], 'dp', split_axis=1, concat_axis=1, tiled=True)  143 us
    psum x1, blocking collectives, shards(): checksums = lax.psum(contribution, ('dp', 'expert'))  68 us
    all_to_all x4, starting transfers between devices, deliver_slots(): lax.all_to_all(send_parts[1], 'dp', split_axis=1, concat_axis=1, tiled=True)  50.7 us
    gather x16, local copies, waits for them, and re-layouts, shards(): source[round_idx][table[round_idx]]  49.8 us
    all_to_all x4, starting transfers between devices, deliver_slots(): lax.all_to_all(send_parts[0], 'dp', split_axis=1, concat_axis=1, tiled=True)  45.9 us
    reduce_sum x1, other arithmetic, shards(): jnp.sum(master_lines * weights, axis=(2, 3)).reshape(round_count * dp_count)  13.4 us
  transfers between devices with their start and end apart: 8, of which 7 were waited for; matrix products, arithmetic and copies ran while one was open for 16% of the time, Pallas kernels for 0%

commit v1 on v0

--- a/solution.py
+++ b/solution.py
@@ -1,13 +1,17 @@
+import functools
 import math
 
 import jax
 import jax.numpy as jnp
 from jax import lax
+from jax.experimental import pallas as pl
+from jax.experimental.pallas import tpu as pltpu
 from jax.sharding import PartitionSpec as P
 
 LANE = 128
 MOST = 3
 STEP = 20
+INNER = 4
 
 
 BETA_ONE = 0.9
@@ -46,11 +50,116 @@
     return 1.0 + pattern.astype(jnp.float32) / 10.0
 
 
-def deliver_slots(send_parts):
-    return (
-        lax.all_to_all(send_parts[0], "dp", split_axis=1, concat_axis=1, tiled=True),
-        lax.all_to_all(send_parts[1], "dp", split_axis=1, concat_axis=1, tiled=True),
-    )
+def exchange_kernel(planes, inner, slots, cap, pos_ref, m_ref, u_ref, om_ref, ou_ref, *scratch):
+    held = scratch[: 2 * planes]
+    stage = scratch[2 * planes : 4 * planes]
+    zs_sem, zr_sem, local_sem, is_sem, ir_sem, self_sem = scratch[4 * planes :]
+    me = lax.axis_index("dp")
+    plane = me // inner
+    spot = me % inner
+    core = lax.axis_index("expert")
+    fields = (m_ref, u_ref)
+    outs = (om_ref, ou_ref)
+
+    def peer(plane_to, spot_to):
+        return (plane_to * inner + spot_to, core)
+
+    barrier = pltpu.get_barrier_semaphore()
+    for d in range(1, planes):
+        pl.semaphore_signal(
+            barrier, inc=1, device_id=peer((plane + d) % planes, spot), device_id_type=pl.DeviceIdType.MESH
+        )
+    for e in range(1, inner):
+        pl.semaphore_signal(
+            barrier, inc=1, device_id=peer(plane, (spot + e) % inner), device_id_type=pl.DeviceIdType.MESH
+        )
+    pl.semaphore_wait(barrier, planes + inner - 2)
+
+    far = [None] * (2 * planes)
+    for f in range(2):
+        own = pltpu.make_async_copy(fields[f].at[plane], held[f * planes], local_sem.at[f])
+        own.start()
+        far[f * planes] = own
+        for d in range(1, planes):
+            to_plane = (plane + d) % planes
+            copy = pltpu.make_async_remote_copy(
+                src_ref=fields[f].at[to_plane],
+                dst_ref=held[f * planes + d],
+                send_sem=zs_sem.at[f * planes + d],
+                recv_sem=zr_sem.at[f * planes + d],
+                device_id=peer(to_plane, spot),
+                device_id_type=pl.DeviceIdType.MESH,
+            )
+            copy.start()
+            far[f * planes + d] = copy
+
+    near = []
+    for f in range(2):
+        for d in range(planes):
+            g = f * planes + d
+            if d == 0:
+                far[g].wait()
+            else:
+                far[g].wait_recv()
+
+            def place(t, carry, g=g):
+                e = t // slots
+                s = t % slots
+                index = pos_ref[(spot + e) % inner, s]
+                found = index < cap
+                lines = held[g][jnp.where(found, index, 0)]
+                stage[g][e, s] = jnp.where(found, lines, 0.0)
+                return carry
+
+            lax.fori_loop(0, inner * slots, place, 0)
+            source = ((plane + planes - d) % planes) * inner + spot
+            for e in range(1, inner):
+                copy = pltpu.make_async_remote_copy(
+                    src_ref=stage[g].at[e],
+                    dst_ref=outs[f].at[:, source],
+                    send_sem=is_sem.at[g * inner + e],
+                    recv_sem=ir_sem.at[g * inner + e],
+                    device_id=peer(plane, (spot + e) % inner),
+                    device_id_type=pl.DeviceIdType.MESH,
+                )
+                copy.start()
+                near.append(copy)
+            copy = pltpu.make_async_copy(stage[g].at[0], outs[f].at[:, source], self_sem.at[g])
+            copy.start()
+            near.append(copy)
+    for f in range(2):
+        for d in range(1, planes):
+            far[f * planes + d].wait_send()
+    for copy in near:
+        copy.wait()
+
+
+def exchange(planes, inner, slots, cap, branch, positions, master_send, update_send):
+    lines, lanes = master_send.shape[2:]
+    shape = jax.ShapeDtypeStruct((slots, planes * inner, lines, lanes), jnp.float32)
+    any_space = pl.BlockSpec(memory_space=pl.ANY)
+    steps = 2 * planes
+    sent = (planes - 1) * cap * 2 * lines * lanes * 4
+    return pl.pallas_call(
+        functools.partial(exchange_kernel, planes, inner, slots, cap),
+        out_shape=(shape, shape),
+        in_specs=[pl.BlockSpec(memory_space=pltpu.SMEM), any_space, any_space],
+        out_specs=(any_space, any_space),
+        scratch_shapes=[pltpu.VMEM((cap, lines, lanes), jnp.float32)] * steps
+        + [pltpu.VMEM((inner, slots, lines, lanes), jnp.float32)] * steps
+        + [
+            pltpu.SemaphoreType.DMA((steps,)),
+            pltpu.SemaphoreType.DMA((steps,)),
+            pltpu.SemaphoreType.DMA((2,)),
+            pltpu.SemaphoreType.DMA((steps * inner,)),
+            pltpu.SemaphoreType.DMA((steps * inner,)),
+            pltpu.SemaphoreType.DMA((steps,)),
+        ],
+        cost_estimate=pl.CostEstimate(flops=0, bytes_accessed=sent * 4, transcendentals=0),
+        compiler_params=pltpu.CompilerParams(
+            collective_id=branch, has_side_effects=True, vmem_limit_bytes=60 * 1024 * 1024
+        ),
+    )(positions, master_send, update_send)
 
 
 def shards(master, first_moment, second_moment, rotation, assignment):
@@ -66,36 +175,57 @@
     piece_len = lines_device // (round_count * dp_count)
     inv_count = 1.0 / math.sqrt(dp_count * piece_len * lane_count)
     table = slot_table(rotation, dp_count, MOST)
-
-    def line_pieces(field_in):
-        return field_in.reshape(round_count, dp_count, piece_len, lane_count)
-
-    def padded_pieces(line_view):
-        return jnp.concatenate(
-            [line_view, jnp.zeros((round_count, 1, piece_len, lane_count), line_view.dtype)], axis=1
-        )
+    span_count = round_count * dp_count
+    inner = INNER
+    planes = dp_count // inner
+    slots = round_count * MOST
+
+    plane_of = rotation.reshape(span_count) // inner
+    span_ids = jnp.arange(span_count, dtype=jnp.int32)
+    same = (plane_of[:, None] == plane_of[None, :]) & (span_ids[None, :] < span_ids[:, None])
+    place_of = jnp.sum(same.astype(jnp.int32), axis=1)
+    plane_ids = jnp.arange(planes, dtype=jnp.int32)
+    loads = jnp.sum((plane_of[None, :] == plane_ids[:, None]).astype(jnp.int32), axis=1)
+    most_load = jnp.max(loads)
+    cap_all = min(inner * slots, span_count)
+    mean_load = span_count // planes
+    caps = sorted({min(cap_all, mean_load * 3 // 2), min(cap_all, mean_load * 2), cap_all})
+    choice = sum((most_load > cap).astype(jnp.int32) for cap in caps[:-1])
+    place_ids = jnp.arange(cap_all, dtype=jnp.int32)
+    listed = (plane_of[None, None, :] == plane_ids[:, None, None]) & (
+        place_of[None, None, :] == place_ids[None, :, None]
+    )
+    lists = jnp.sum(listed.astype(jnp.int32) * span_ids, axis=2)
+    mine = table.transpose(2, 0, 1).reshape(planes, inner, round_count, MOST)
+    mine = lax.dynamic_index_in_dim(mine, position // inner, 0, keepdims=False)
+    padded_place = jnp.concatenate(
+        [place_of.reshape(round_count, dp_count), jnp.full((round_count, 1), cap_all, jnp.int32)], axis=1
+    )
+    hits = mine[..., None] == jnp.arange(dp_count + 1, dtype=jnp.int32)
+    positions = jnp.sum(hits * padded_place[None, :, None, :], axis=3).reshape(inner, slots)
 
     update = scaled_moment(first_moment, second_moment)
-    master_lines = line_pieces(master)
-    update_lines = line_pieces(update)
+    master_lines = master.reshape(span_count, piece_len, lane_count)
+    update_lines = update.reshape(span_count, piece_len, lane_count)
     local_lines = position * lines_device + jnp.arange(lines_device, dtype=jnp.int32).reshape(
-        round_count, dp_count, piece_len
+        span_count, piece_len
     )
     weights = position_weights(local_lines, per_row, lane_count)
-    master_sums = (
-        jnp.sum(master_lines * weights, axis=(2, 3)).reshape(round_count * dp_count) * inv_count
-    )
-    update_sums = (
-        jnp.sum(update_lines * weights, axis=(2, 3)).reshape(round_count * dp_count) * inv_count
-    )
-    sources = (padded_pieces(master_lines), padded_pieces(update_lines))
-    results = []
-    for round_idx in range(round_count):
-        send_parts = tuple((source[round_idx][table[round_idx]] for source in sources))
-        results.append(deliver_slots(send_parts))
-    saved_master = jnp.stack([outcome[0] for outcome in results])
-    saved_update = jnp.stack([outcome[1] for outcome in results])
-    span_count = assignment.shape[0]
+    master_sums = jnp.sum(master_lines * weights, axis=(1, 2)) * inv_count
+    update_sums = jnp.sum(update_lines * weights, axis=(1, 2)) * inv_count
+
+    def branch_of(number, cap):
+        def run(master_in, update_in):
+            chosen = lists[:, :cap]
+            return exchange(
+                planes, inner, slots, cap, number, positions, master_in[chosen], update_in[chosen]
+            )
+
+        return run
+
+    saved_master, saved_update = lax.switch(
+        choice, [branch_of(number, cap) for number, cap in enumerate(caps)], master_lines, update_lines
+    )
     slot_ids = jnp.arange(span_count, dtype=jnp.int32)
     permuting = (assignment[:, None] == slot_ids[None, :]).astype(jnp.float32)
     both_sums = jnp.stack([master_sums, update_sums])

time: 606 us -> 436 us (0.72)
  waiting for transfers between devices: 318 us -> 0 us
  Pallas kernels: 0 us -> 276 us
  starting transfers between devices: 96.6 us -> 0 us
  local copies, waits for them, and re-layouts: 88 us -> 36.5 us
  blocking collectives: 68 us -> 95.1 us
  other arithmetic: 32.6 us -> 24.6 us
    all_to_all x8 -> x0, waiting for transfers between devices: 318 us -> none  [the longest x4 175 us: deliver_slots(): lax.all_to_all(send_parts[0], 'dp', split_axis=1, concat_axis=1, tiled=True)]
    pallas_call x0 -> x1, Pallas kernels: none -> 276 us  [exchange(): pl.pallas_call(functools.partial(exchange_kernel, planes, inner, slots, c...]
    all_to_all x8 -> x0, starting transfers between devices: 96.6 us -> none  [the longest x4 50.7 us: deliver_slots(): lax.all_to_all(send_parts[1], 'dp', split_axis=1, concat_axis=1, tiled=True)]
    gather x16 -> x2, local copies, waits for them, and re-layouts: 49.8 us -> 10.8 us  [the longest x1 5.38 us: run(): master_in[chosen]]
    psum x1, blocking collectives: 68 us -> 95.1 us  [shards(): checksums = lax.psum(contribution, ('dp', 'expert'))]
    all_to_all x8 -> x0, local copies, waits for them, and re-layouts: 18.9 us -> none  [the longest x4 11 us: deliver_slots(): lax.all_to_all(send_parts[1], 'dp', split_axis=1, concat_axis=1, tiled=True)]
    unnamed x8 -> x13, local copies, waits for them, and re-layouts: 2.41 us -> 14.1 us
    another operation x2 -> x0, other arithmetic: 10.2 us -> none  [the longest x1 5.67 us: shards(): saved_update = jnp.stack([outcome[1] for outcome in results])]
  transfers between devices with their start and end apart: 8 -> 0, of which waited for: 7 -> 0; matrix products, arithmetic and copies ran while one was open for 16% -> 0% of each run, Pallas kernels for 0% -> 0%
where the time goes in v1:
time: 436 us; the launch traced here: 435 us
  Pallas kernels  276 us (63%)
  blocking collectives  95.1 us (22%)
  local copies, waits for them, and re-layouts  36.5 us (8%)
  other arithmetic  24.6 us (6%)
    pallas_call x1, Pallas kernels, exchange(): pl.pallas_call(functools.partial(exchange_kernel, planes, inner, slots, c...  276 us
    psum x1, blocking collectives, shards(): checksums = lax.psum(contribution, ('dp', 'expert'))  95.1 us
    unnamed x13, local copies, waits for them, and re-layouts  14.1 us
    reduce_sum x1, other arithmetic, shards(): master_sums = jnp.sum(master_lines * weights, axis=(1, 2)) * inv_count  13.6 us

profile of v1, /device:TPU:0, one launch (start us, length us, event | category | flops | bytes accessed | tf_op | source)
XLA Modules:
  0.0 434.9 jit_solution(2494797706777970908)
XLA Ops:
  0.6 0.7 iota_compare_fusion.2
  1.3 1.0 convert_reduce_fusion.1
  2.3 0.5 fusion.13
  2.8 0.8 reshape.383
  3.6 6.4 %add_divide_fusion = f32[1,448,2048]{2,1,0:T(8,128)} fusion(f32[1,448,2048]{2,1,0:T(8,128)} %param.10, f32[1,448,2048]{2,1,0:T(8,128)} %param.9), kind=kLoop, calls=%fused_computation.54 | loop fusion | flops 3670016 | bytes 11010048 | tf_op jit(solution)/shard_map/div | solution.py:25
  10.0 4.7 %reshape.385 = f32[64,112,128]{2,1,0:T(8,128)} reshape(f32[1,448,2048]{2,1,0:T(8,128)} %add_divide_fusion) | data formatting | bytes 7340032 | tf_op jit(solution)/shard_map/reshape | solution.py:209
  14.8 4.8 %reshape.384 = f32[64,112,128]{2,1,0:T(8,128)} reshape(f32[1,448,2048]{2,1,0:T(8,128)} %param.8) | data formatting | bytes 7340032 | tf_op jit(solution)/shard_map/reshape | solution.py:208
  19.6 0.5 broadcast.553
  20.1 0.7 reduce.5
  20.8 0.1 reshape.382
  20.9 0.2 convert_reduce_fusion
  21.1 0.1 convert_reduce_fusion.2
  21.2 0.6 reduce_max.9
  23.2 289.0 %conditional.1 = (f32[1,4,3,1792,128]{4,3,2,1,0:T(8,128)}, f32[1,4,3,1792,128]{4,3,2,1,0:T(8,128)}) conditional(s32[]{:T(128)} %clamp.3, (s32[16,4,3]{0,2,1:T(4,128)S(1)}, s32[16,4,3]{0,2,1:T(4,128)S(1)}, s32[]{:T(128)}, s32[4,4,3,17]{3,1,2,0:T(4,128)S(1)}, s32[64]{0:T(128)S(1)}, /*index=5*/s32[1,1,64]{2,1,0:T(1,128)S(1)}, ...), branch_computations={%region_6.0_spmd, %region_9.12_spmd, %region_12.15_spmd} | conditional | flops 45091 | bytes 110192088 | solution.py:226
  23.2 0.1 reshape.360
  23.3 0.1 copy.47
  23.4 0.1 reshape.361
  23.5 0.4 select_reduce_fusion.1
  23.9 0.1 copy.31
  24.0 0.7 reshape.362.pos_ref
  24.7 0.1 select_reduce_fusion
  24.9 0.1 reshape.391
  24.9 5.4 %gather_fusion = f32[96,112,128]{2,1,0:T(8,128)} fusion(f32[64,112,128]{2,1,0:T(8,128)} %get-tuple-element.466, s32[1024]{0:T(1024)S(1)} %pad_clamp_fusion), kind=kCustom, calls=%fused_computation | custom fusion | bytes 11010432 | tf_op jit(solution)/shard_map/cond/branch_0_fun/gather | solution.py:221
  30.3 5.4 %gather_fusion.1 = f32[96,112,128]{2,1,0:T(8,128)} fusion(f32[64,112,128]{2,1,0:T(8,128)} %get-tuple-element.475, s32[1024]{0:T(1024)S(1)} %pad_clamp_fusion), kind=kCustom, calls=%fused_computation.1 | custom fusion | bytes 11010432 | tf_op jit(solution)/shard_map/cond/branch_0_fun/gather | solution.py:221
  35.7 276.5 %branch_0_fun.2 = (f32[12,16,112,128]{3,2,1,0:T(8,128)}, f32[12,16,112,128]{3,2,1,0:T(8,128)}) custom-call(s32[4,12]{1,0:T(4,128)} %reshape.362.pos_ref, f32[4,24,112,128]{3,2,1,0:T(8,128)} %bitcast.59, f32[4,24,112,128]{3,2,1,0:T(8,128)} %bitcast.60), custom_call_target="tpu_custom_call" | custom-call | bytes 33030144 | tf_op jit(solution)/shard_map/cond/branch_0_fun/pallas_call | solution.py:143
  312.3 13.6 %multiply_reduce_fusion.1 = (f32[64]{0:T(128)S(1)}, f32[64]{0:T(128)S(1)}) fusion(f32[64,112,128]{2,1,0:T(8,128)} %reshape.384, s32[64,112]{1,0:T(8,128)S(1)} %get-tuple-element.571, s32[64,112]{1,0:T(8,128)S(1)} %get-tuple-element.570, f32[64,112,128]{2,1,0:T(8,128)} %reshape.385), kind=kLoop, calls=%fused_computation.50 | loop fusion | flops 14679936 | bytes 7397888 | tf_op jit(solution)/shard_map/reduce_sum | solution.py:214
  325.9 0.1 fusion.19
  326.0 0.1 multiply_reduce_fusion.2
  326.1 0.1 broadcast_multiply_fusion
  326.2 95.1 %psum.7 = f32[2,2,64]{2,1,0:T(2,128)} all-reduce(f32[2,2,64]{2,1,0:T(2,128)S(1)} %broadcast_multiply_fusion), channel_id=1, replica_groups=mesh['dp'=16,'expert'=2] {'dp','expert'}, use_global_device_ids=true, to_apply=%region_18.19 | all-reduce | flops 256 | bytes 2048 | tf_op jit(solution)/shard_map/psum | solution.py:235
  421.3 9.3 %copy.76 = f32[1,4,3,1792,128]{4,3,2,1,0:T(8,128)} copy(f32[1,4,3,1792,128]{4,3,2,1,0:T(8,128)} %get-tuple-element.581) | data formatting | bytes 22020096
  430.6 4.3 copy.77
  (34 shorter events, 0.2 us)
Async XLA Ops:
  14.8 5.3 %copy-start = (s32[4,16,1]{1,2,0:T(1,128)S(1)}, s32[4,16,1]{1,2,0:T(1,128)}, u32[]{:S(2)}) copy-start(s32[4,16,1]{1,2,0:T(1,128)} %param.11) | copy-start | bytes 772
  312.3 13.6 %copy-start.1 = (s32[64]{0:T(128)S(1)}, s32[64]{0:T(128)}, u32[]{:S(2)}) copy-start(s32[64]{0:T(128)} %param.12) | copy-start | bytes 772
  312.3 118.3 %slice-start = ((s8[11010048]{0:T(1024)(128)(4,1)}), s8[2621440]{0:T(1024)(128)(4,1)S(1)}, s32[]{:S(2)}) async-start(s8[11010048]{0:T(1024)(128)(4,1)} %bitcast.67), calls=%async_computation | async-start | bytes 5242880
  421.3 9.3 %slice-start.1 = ((s8[11010048]{0:T(1024)(128)(4,1)}), s8[4194304]{0:T(1024)(128)(4,1)S(1)}, s32[]{:S(2)}) async-start(s8[11010048]{0:T(1024)(128)(4,1)} %bitcast.67), calls=%async_computation.1 | async-start | bytes 8388608
  421.3 9.3 %slice-start.2 = ((s8[11010048]{0:T(1024)(128)(4,1)}), s8[4194304]{0:T(1024)(128)(4,1)S(1)}, s32[]{:S(2)}) async-start(s8[11010048]{0:T(1024)(128)(4,1)} %bitcast.67), calls=%async_computation.2 | async-start | bytes 8388608
